TPU v7x, 32 devices: a whole 2x2x4 slice. The times are simulated.
32 devices in a mesh: pipe: 4 (over y, core), tensor: 8 (over z, x).
Axes of the slice: x: 2, y: 2, z: 4, core: 2. Of those that a mesh axis runs over, the one named last changes fastest.
Arguments:
- patches: bfloat16 [16384, 1280], P(('pipe', 'tensor')), may hold values from -6 to 6
- attn_gain: float32 [1280], replicated, may hold values from 0.25 to 1.75
- w_qkv: bfloat16 [1280, 3840], P('tensor', 'pipe'), may hold values from -0.1118034 to 0.1118034
- w_out: bfloat16 [1280, 1280], P('tensor', 'pipe'), may hold values from -0.15625 to 0.15625
- merge_gain: float32 [1280], replicated, may hold values from 0.25 to 1.75
- window_ids: int32 [16384], P(('pipe', 'tensor')), may hold values from 0 to 127, as said below
- image_patches: int32 [128], P(('pipe', 'tensor')), may hold values from 0 to 512, as said below
- image_sample: int32 [128], P(('pipe', 'tensor')), may hold values from 0 to 7
Outputs:
- vision_seq: bfloat16 [4, 128, 8, 5120], P('pipe', None, 'tensor')
Inputs may be any that keep to these rules, and one draw needn't show every extreme that they name: `window_ids`: Non-decreasing within each bundle and equal over each 4 consecutive slots; every window lies within one aligned block of 64 slots of a bundle. `image_patches`: multiples of 128; the images of one bundle take at most 512 slots and at least half of them, and in every micro-batch some bundle is full.
All inputs are finite; a program needn't handle non-finite values.
Results may differ from a plain program's by a relative error of at most 0.0053.
Values may be sent and summed in bfloat16 or wider, within the bound.
A program may use at most 64 MiB of HBM per device.

v0:
```python
import math
import jax
import jax.numpy as jnp
from jax import lax
from jax.sharding import PartitionSpec as P

HEADS = 16
WINDOW = 64
SAMPLES = 8
epsilon = 1e-06


def normalize(values, gain_row):
    return (
        values * lax.rsqrt(jnp.mean(values * values, axis=-1, keepdims=True) + epsilon) * gain_row
    )


def token_positions(starts, merged_count, token_count):
    offsets = jnp.cumsum(merged_count) - merged_count
    token_index = jnp.arange(token_count, dtype=jnp.int32)
    inside = (token_index[None, :] >= offsets[:, None]) & (
        token_index[None, :] < (offsets + merged_count)[:, None]
    )
    position = jnp.sum(
        jnp.where(inside, starts[:, None] + token_index[None, :] - offsets[:, None], 0), axis=0
    )
    return jnp.where(jnp.any(inside, axis=0), position, -1)


def body(patches, attn_gain, w_qkv, w_out, merge_gain, window_ids, image_patches, image_sample):
    patch_count, feature_width = patches.shape
    token_count = patch_count // 4
    group_size = lax.axis_size("tensor")
    own_index = lax.axis_index("tensor")
    residual = patches.astype(jnp.float32)
    normed = normalize(residual, attn_gain).astype(jnp.bfloat16)
    qkv_rows = lax.all_gather(w_qkv, "tensor", axis=0, tiled=True)
    qkv = jnp.dot(
        normed,
        lax.all_gather(qkv_rows, "pipe", axis=1, tiled=True),
        preferred_element_type=jnp.float32,
    ).astype(jnp.bfloat16)
    head_width = feature_width // HEADS
    tile_count = patch_count // WINDOW

    def split_heads(block):
        return block.reshape(tile_count, WINDOW, HEADS, head_width)

    queries = split_heads(qkv[:, :feature_width])
    keys_tile = split_heads(qkv[:, feature_width : 2 * feature_width])
    values_tile = split_heads(qkv[:, 2 * feature_width :])
    scores = jnp.einsum(
        "tqhd,tkhd->thqk", queries, keys_tile, preferred_element_type=jnp.float32
    ) * (1.0 / math.sqrt(head_width))
    live_row = jnp.arange(patch_count, dtype=jnp.int32) < jnp.sum(image_patches)
    window_tile = window_ids.reshape(tile_count, WINDOW)
    live_tile = live_row.reshape(tile_count, WINDOW)
    allowed = (window_tile[:, :, None] == window_tile[:, None, :]) & live_tile[:, None, :]
    scores = jnp.where(allowed[:, None, :, :], scores, -1e30)
    row_max = jnp.max(scores, axis=-1, keepdims=True)
    exponent = jnp.exp(scores - row_max)
    weights = (exponent / jnp.sum(exponent, axis=-1, keepdims=True)).astype(jnp.bfloat16)
    context = jnp.einsum(
        "thqk,tkhd->tqhd", weights, values_tile, preferred_element_type=jnp.float32
    ).reshape(patch_count, feature_width)
    context = jnp.where(live_row[:, None], context, 0.0).astype(jnp.bfloat16)
    proj_rows = lax.all_gather(w_out, "tensor", axis=0, tiled=True)
    attended = jnp.dot(
        context,
        lax.all_gather(proj_rows, "pipe", axis=1, tiled=True),
        preferred_element_type=jnp.float32,
    )
    hidden = residual + attended
    merged = (
        normalize(hidden, merge_gain).astype(jnp.bfloat16).reshape(token_count, 4 * feature_width)
    )
    outgoing = merged.reshape(token_count // group_size, group_size, 4 * feature_width)
    merged_count = image_patches // 4
    sample_hot = image_sample[:, None] == jnp.arange(SAMPLES, dtype=jnp.int32)[None, :]
    sample_tally = jnp.sum(jnp.where(sample_hot, merged_count[:, None], 0), axis=0)
    all_tallies = lax.all_gather(sample_tally[None, :], "tensor", axis=0, tiled=True)
    source_ranks = jnp.arange(group_size, dtype=jnp.int32)
    before = jnp.sum(jnp.where((source_ranks < own_index)[:, None], all_tallies, 0), axis=0)
    totals = jnp.sum(all_tallies, axis=0)
    sample_index = jnp.arange(SAMPLES, dtype=jnp.int32)
    sample_base = jnp.sum(
        jnp.where(sample_index[None, :] < sample_index[:, None], totals[None, :], 0), axis=1
    )
    image_order = jnp.arange(image_sample.shape[0], dtype=jnp.int32)
    same_before = (image_sample[None, :] == image_sample[:, None]) & (
        image_order[None, :] < image_order[:, None]
    )
    earlier = jnp.sum(jnp.where(same_before, merged_count[None, :], 0), axis=1)
    starts = jnp.sum(jnp.where(sample_hot, (sample_base + before)[None, :], 0), axis=1) + earlier
    position = token_positions(starts, merged_count, token_count)
    outgoing_position = position.reshape(token_count // group_size, group_size)
    received, received_position = (
        lax.all_to_all(outgoing, "tensor", split_axis=1, concat_axis=0, tiled=True),
        lax.all_to_all(outgoing_position, "tensor", split_axis=1, concat_axis=0, tiled=True),
    )
    dest_rows = received_position.reshape(token_count) // group_size
    placement = (jnp.arange(token_count, dtype=jnp.int32)[:, None] == dest_rows[None, :]).astype(
        jnp.bfloat16
    )
    placed = jnp.dot(
        placement,
        received.reshape(token_count, 4 * feature_width),
        preferred_element_type=jnp.float32,
    )
    return placed.astype(jnp.bfloat16).reshape(1, token_count, 1, 4 * feature_width)


def solution(mesh):
    return jax.shard_map(
        body,
        mesh=mesh,
        in_specs=(
            P(("pipe", "tensor"), None),
            P(),
            P("tensor", "pipe"),
            P("tensor", "pipe"),
            P(),
            P(("pipe", "tensor")),
            P(("pipe", "tensor")),
            P(("pipe", "tensor")),
        ),
        out_specs=P("pipe", None, "tensor", None),
        check_vma=False,
    )
```

profile of v0, /device:TPU:0, one launch (start us, length us, event | category | flops | bytes accessed | tf_op | source)
XLA Modules:
  0.0 223.8 jit_solution(180956799762831658)
XLA Ops:
  6.5 0.7 all-gather.5.cloned.1.call-update
  7.3 0.0 all-gather.7.cloned.1.call-start
  7.3 59.4 %all-gather.5.cloned.1.call-done = bf16[1280,960]{1,0:T(8,128)(2,1)} async-done(((bf16[160,960]{1,0:T(8,128)(2,1)}), bf16[1280,960]{1,0:T(8,128)(2,1)}) %all-gather.5.cloned.1.call-update) | async-done | bytes 2457616 | tf_op jit(solution)/shard_map/all_gather | solution.py:38
  66.7 4.4 %copy.40 = bf16[1280,960]{0,1:T(8,128)(2,1)} copy(bf16[1280,960]{1,0:T(8,128)(2,1)} %all-gather.5.cloned.1.call-done) | data formatting | bytes 4915200 | tf_op jit(solution)/shard_map/all_gather | solution.py:38
  71.1 0.0 all-gather.9.cloned.1.call-start
  71.2 33.0 %all_gather.18 = bf16[1280,320]{1,0:T(8,128)(2,1)S(1)} all-gather(bf16[160,320]{1,0:T(8,128)(2,1)S(1)} %copy-done.3), channel_id=1, replica_groups=mesh['pipe'=4,'tensor'=8] {'tensor'}, dimensions={0}, use_global_device_ids=true | all-gather | bytes 921600 | tf_op jit(solution)/shard_map/all_gather | solution.py:68
  104.2 1.3 copy.46
  105.5 0.6 and_select_fusion.1
  106.1 0.1 select_reduce_fusion.5
  106.2 0.2 select_reduce_fusion.3
  106.4 0.6 dynamic-slice
  107.7 0.2 dynamic-update-slice
  108.0 8.6 %all-reduce = s32[64]{0:T(128)S(1)} all-reduce(s32[64]{0:T(128)S(1)} %dynamic-update-slice), channel_id=2, replica_groups=mesh['pipe'=4,'tensor'=8] {'tensor'}, use_global_device_ids=true, to_apply=%add | all-reduce | flops 64 | bytes 512
  116.6 0.1 reshape.163
  116.6 0.1 select_reduce_fusion
  116.7 0.1 select_reduce_fusion.1
  116.8 0.2 reduce-window.8
  117.0 0.2 select_reduce_fusion.4
  117.2 0.1 fusion.25
  117.3 0.1 select_reduce_fusion.2
  117.4 0.1 select_n.69
  117.5 0.7 copy.39
  118.2 4.5 %all-to-all-start = ((s32[16,8,1]{0,2,1:T(1,128)}), s32[16,8,1]{0,2,1:T(1,128)S(1)}, u32[]{:S(2)}, u32[]{:S(2)}) async-start(s32[16,8,1]{0,2,1:T(1,128)} %copy.39), calls=%async_computation | async-start | bytes 8192 | tf_op jit(solution)/shard_map/all_to_all | solution.py:100
  122.7 0.1 eq.67
  122.8 0.6 iota_compare_fusion.3
  123.5 0.7 add_compare_fusion
  124.1 0.3 fusion.3
  124.5 0.2 compare_and_fusion
  124.7 11.6 %all-gather.7.cloned.1.call-done = bf16[1280,3840]{0,1:T(8,128)(2,1)} async-done(((bf16[1280,960]{0,1:T(8,128)(2,1)}), bf16[1280,3840]{0,1:T(8,128)(2,1)}) %all-gather.7.cloned.1.call-update) | async-done | bytes 9830416 | tf_op jit(solution)/shard_map/all_gather | solution.py:41
  136.3 9.5 %convolution_convert_fusion.1 = bf16[512,3840]{1,0:T(8,128)(2,1)S(1)} fusion(bf16[1280,3840]{0,1:T(8,128)(2,1)} %all-gather.7.cloned.1.call-done, bf16[512,1280]{1,0:T(8,128)(2,1)S(1)} %copy-done.1, f32[1280]{0:T(1024)S(1)} %copy-done.7, f32[512]{0:T(512)S(1)} %add_rsqrt_fusion.1), kind=kOutput, calls=%fused_computation.2 | convolution fusion | flops 5037752320 | bytes 15080448 | tf_op jit(solution)/shard_map/dot_general | solution.py:39
  145.8 1.7 fusion.26
  147.5 4.1 %reshape.158 = bf16[8,64,16,80]{3,2,1,0:T(8,128)(2,1)S(1)} reshape(bf16[512,1280]{1,0:T(8,128)(2,1)} %get-tuple-element.9) | data formatting | bytes 2621440 | tf_op jit(solution)/shard_map/reshape | solution.py:48
  151.6 5.0 %reshape.159 = bf16[8,64,16,80]{3,2,1,0:T(8,128)(2,1)} reshape(bf16[512,1280]{1,0:T(8,128)(2,1)} %get-tuple-element.8) | data formatting | bytes 2621440 | tf_op jit(solution)/shard_map/reshape | solution.py:48
  156.7 4.1 %reshape.157 = bf16[8,64,16,80]{3,2,1,0:T(8,128)(2,1)} reshape(bf16[512,1280]{1,0:T(8,128)(2,1)S(1)} %get-tuple-element.7) | data formatting | bytes 2621440 | tf_op jit(solution)/shard_map/reshape | solution.py:48
  160.8 2.8 %fusion.7 = f32[8,16,64,64]{2,3,1,0:T(8,128)S(1)} fusion(bf16[8,64,16,80]{3,2,1,0:T(8,128)(2,1)} %reshape.159, bf16[8,64,16,80]{3,2,1,0:T(8,128)(2,1)S(1)} %reshape.158), kind=kOutput, calls=%fused_computation.19 | convolution fusion | flops 83886080 | bytes 4718592 | tf_op jit(solution)/shard_map/tqhd,tkhd->thqk/dot_general | solution.py:53
  163.6 1.5 fusion.27
  165.1 0.1 copy-done
  165.2 1.2 convolution_bitcast_fusion
  166.4 1.4 copy.45
  167.8 3.3 %reshape.160 = bf16[512,1280]{1,0:T(8,128)(2,1)} reshape(bf16[8,64,16,80]{3,2,1,0:T(8,128)(2,1)S(1)} %copy.45) | data formatting | bytes 2621440 | tf_op jit(solution)/shard_map/reshape | solution.py:66
  171.1 4.3 %multiply_reduce_fusion = (f32[512]{0:T(512)S(1)}, f32[512,1280]{1,0:T(8,128)S(1)}) fusion(bf16[1280,1280]{0,1:T(8,128)(2,1)} %all-gather.9.cloned.1.call-done, bf16[512,1280]{1,0:T(8,128)(2,1)} %reshape.160, pred[512]{0:T(512)(128)(4,1)S(1)} %iota_compare_fusion.3, bf16[512,1280]{1,0:T(8,128)(2,1)S(1)} %copy-done.2), kind=kOutput, calls=%fused_computation.15 | convolution fusion | flops 1680997888 | bytes 8522240 | tf_op jit(solution)/shard_map/dot_general | solution.py:69
  175.4 0.3 multiply_convert_fusion
  175.7 0.8 reshape_reshape.3
  176.6 1.8 copy.47
  178.3 5.5 %all-to-all-start.1 = ((bf16[16,8,5120]{2,0,1:T(8,128)(2,1)}), bf16[16,8,5120]{2,0,1:T(8,128)(2,1)S(1)}, u32[]{:S(2)}, u32[]{:S(2)}) async-start(bf16[16,8,5120]{2,0,1:T(8,128)(2,1)} %copy.47), calls=%async_computation.1 | async-start | bytes 2621440 | tf_op jit(solution)/shard_map/all_to_all | solution.py:99
  183.9 0.1 reshape.156
  184.0 31.7 %all-to-all-done.1 = bf16[16,8,5120]{2,0,1:T(8,128)(2,1)S(1)} async-done(((bf16[16,8,5120]{2,0,1:T(8,128)(2,1)}), bf16[16,8,5120]{2,0,1:T(8,128)(2,1)S(1)}, u32[]{:S(2)}, u32[]{:S(2)}) %all-to-all-start.1) | async-done | bytes 1310752 | tf_op jit(solution)/shard_map/all_to_all | solution.py:99
  215.7 1.6 fusion.1
  (34 shorter events, 0.2 us)
Async XLA Ops:
  6.5 60.1 %all-gather.5.cloned.1.call-start = ((), (), s32[]{:S(2)}) async-start(), calls=%async_computation.2 | async-start | bytes 2949120 | tf_op jit(solution)/shard_map/all_gather | solution.py:38
  7.3 63.9 %copy-start.3 = (bf16[160,320]{1,0:T(8,128)(2,1)S(1)}, bf16[160,320]{1,0:T(8,128)(2,1)}, u32[]{:S(2)}) copy-start(bf16[160,320]{1,0:T(8,128)(2,1)} %param.11) | copy-start | bytes 307204
  7.3 129.0 %all-gather.7.cloned.1.call-start = ((), (), s32[]{:S(2)}) async-start(), calls=%async_computation.3 | async-start | bytes 12288000 | tf_op jit(solution)/shard_map/all_gather | solution.py:41
  71.0 34.4 %copy-start.8 = (s32[4]{0:T(128)S(1)}, s32[4]{0:T(128)}, u32[]{:S(2)}) copy-start(s32[4]{0:T(128)} %param.14) | copy-start | bytes 52
  71.0 35.1 %copy-start.6 = (s32[4]{0:T(128)S(1)}, s32[4]{0:T(128)}, u32[]{:S(2)}) copy-start(s32[4]{0:T(128)} %param.15) | copy-start | bytes 52
  71.0 35.4 %copy-start.9 = (u32[32]{0:T(128)S(1)}, u32[32]{0:T(128)}, u32[]{:S(2)}) copy-start(u32[32]{0:T(128)} %constant.61) | copy-start | bytes 388
  71.1 51.7 %copy-start.5 = (s32[512]{0:T(512)S(1)}, s32[512]{0:T(512)}, u32[]{:S(2)}) copy-start(s32[512]{0:T(512)} %param.13) | copy-start | bytes 6148
  71.1 53.1 %copy-start.1 = (bf16[512,1280]{1,0:T(8,128)(2,1)S(1)}, bf16[512,1280]{1,0:T(8,128)(2,1)}, u32[]{:S(2)}) copy-start(bf16[512,1280]{1,0:T(8,128)(2,1)} %param.8) | copy-start | bytes 3932164
  71.1 65.2 %copy-start.7 = (f32[1280]{0:T(1024)S(1)}, f32[1280]{0:T(1024)}, u32[]{:S(2)}) copy-start(f32[1280]{0:T(1024)} %param.9) | copy-start | bytes 15364
  71.1 99.9 %all-gather.9.cloned.1.call-start = ((), (), s32[]{:S(2)}) async-start(), calls=%async_computation.4 | async-start | bytes 4096000 | tf_op jit(solution)/shard_map/all_gather | solution.py:71
  118.2 60.2 %all-to-all-start = ((s32[16,8,1]{0,2,1:T(1,128)}), s32[16,8,1]{0,2,1:T(1,128)S(1)}, u32[]{:S(2)}, u32[]{:S(2)}) async-start(s32[16,8,1]{0,2,1:T(1,128)} %copy.39), calls=%async_computation | async-start | bytes 8192 | tf_op jit(solution)/shard_map/all_to_all | solution.py:100
  163.6 1.6 copy-start
  167.8 3.3 %copy-start.2 = (bf16[512,1280]{1,0:T(8,128)(2,1)S(1)}, bf16[512,1280]{1,0:T(8,128)(2,1)}, u32[]{:S(2)}) copy-start(bf16[512,1280]{1,0:T(8,128)(2,1)} %param.8) | copy-start | bytes 3932164
  171.1 4.4 %copy-start.4 = (f32[1280]{0:T(1024)S(1)}, f32[1280]{0:T(1024)}, u32[]{:S(2)}) copy-start(f32[1280]{0:T(1024)} %param.12) | copy-start | bytes 15364
  178.3 37.3 %all-to-all-start.1 = ((bf16[16,8,5120]{2,0,1:T(8,128)(2,1)}), bf16[16,8,5120]{2,0,1:T(8,128)(2,1)S(1)}, u32[]{:S(2)}, u32[]{:S(2)}) async-start(bf16[16,8,5120]{2,0,1:T(8,128)(2,1)} %copy.47), calls=%async_computation.1 | async-start | bytes 2621440 | tf_op jit(solution)/shard_map/all_to_all | solution.py:99
Sparse Core Ops, SparseCore 0:
  9.5 57.1 all-gather.4
  71.2 65.0 all-gather.6
  137.8 29.2 all-gather.8
where the time goes:
time: 224 us
  waiting for transfers between devices  103 us (46%)
  blocking collectives  41.6 us (19%)
  local copies, waits for them, and re-layouts  29.9 us (13%)
  matrix products  19.4 us (9%)
  between operations  14 us (6%)
  starting transfers between devices  10.1 us (5%)
  other arithmetic  5.32 us (2%)
    all_gather x1, waiting for transfers between devices, body(): qkv_rows = lax.all_gather(w_qkv, 'tensor', axis=0, tiled=True)  59.4 us
    all_gather x1, blocking collectives, body(): proj_rows = lax.all_gather(w_out, 'tensor', axis=0, tiled=True)  33 us
    all_to_all x1, waiting for transfers between devices, body(): lax.all_to_all(outgoing, 'tensor', split_axis=1, concat_axis=0, tiled=True)  31.7 us
    reshape x3, local copies, waits for them, and re-layouts, split_heads(): return block.reshape(tile_count, WINDOW, HEADS, head_width)  13.2 us
    all_gather x1, waiting for transfers between devices, body(): lax.all_gather(qkv_rows, 'pipe', axis=1, tiled=True)  11.6 us
    dot_general x1, matrix products, body(): jnp.dot(normed, lax.all_gather(qkv_rows, 'pipe', axis=1, tiled=True), pre...  9.49 us
    unnamed x1, blocking collectives  8.57 us
    all_to_all x1, starting transfers between devices, body(): lax.all_to_all(outgoing, 'tensor', split_axis=1, concat_axis=0, tiled=True)  5.51 us
  transfers between devices with their start and end apart: 5, of which 3 were waited for; matrix products, arithmetic and copies ran while one was open for 22% of the time, Pallas kernels for 0%

commit v1 on v0

--- a/solution.py
+++ b/solution.py
@@ -38,7 +38,7 @@
     qkv_rows = lax.all_gather(w_qkv, "tensor", axis=0, tiled=True)
     qkv = jnp.dot(
         normed,
-        lax.all_gather(qkv_rows, "pipe", axis=1, tiled=True),
+        jnp.concatenate(lax.all_gather(qkv_rows, "pipe"), 1),
         preferred_element_type=jnp.float32,
     ).astype(jnp.bfloat16)
     head_width = feature_width // HEADS

time: 224 us -> 250 us (1.12)
  local copies, waits for them, and re-layouts: 29.9 us -> 50.1 us
  waiting for transfers between devices: 103 us -> 109 us
    all_gather x1, local copies, waits for them, and re-layouts: 4.38 us -> 17.1 us  [body(): lax.all_gather(qkv_rows, 'pipe')]
    reshape x0 -> x1, local copies, waits for them, and re-layouts: none -> 8.88 us  [body(): jnp.concatenate(lax.all_gather(qkv_rows, 'pipe'), 1)]
    all_gather x1, waiting for transfers between devices: 11.6 us -> 16.9 us  [body(): lax.all_gather(qkv_rows, 'pipe')]
  transfers between devices with their start and end apart: 5 -> 5, of which waited for: 3 -> 3; matrix products, arithmetic and copies ran while one was open for 22% -> 29% of each run, Pallas kernels for 0% -> 0%
where the time goes in v1:
time: 250 us; the launch traced here: 249 us
  waiting for transfers between devices  109 us (44%)
  local copies, waits for them, and re-layouts  50.1 us (20%)
  blocking collectives  41.6 us (17%)
  matrix products  19.4 us (8%)
  between operations  13.9 us (6%)
  starting transfers between devices  10 us (4%)
  other arithmetic  5.5 us (2%)
    all_gather x1, waiting for transfers between devices, body(): qkv_rows = lax.all_gather(w_qkv, 'tensor', axis=0, tiled=True)  59.4 us
    all_gather x1, blocking collectives, body(): proj_rows = lax.all_gather(w_out, 'tensor', axis=0, tiled=True)  33 us
    all_to_all x1, waiting for transfers between devices, body(): lax.all_to_all(outgoing, 'tensor', split_axis=1, concat_axis=0, tiled=True)  31.7 us
    all_gather x1, local copies, waits for them, and re-layouts, body(): lax.all_gather(qkv_rows, 'pipe')  17.1 us
    all_gather x1, waiting for transfers between devices, body(): lax.all_gather(qkv_rows, 'pipe')  16.9 us
    reshape x3, local copies, waits for them, and re-layouts, split_heads(): return block.reshape(tile_count, WINDOW, HEADS, head_width)  12.3 us
    dot_general x1, matrix products, body(): jnp.dot(normed, jnp.concatenate(lax.all_gather(qkv_rows, 'pipe'), 1), pre...  9.52 us
    reshape x1, local copies, waits for them, and re-layouts, body(): jnp.concatenate(lax.all_gather(qkv_rows, 'pipe'), 1)  8.88 us
  transfers between devices with their start and end apart: 5, of which 3 were waited for; matrix products, arithmetic and copies ran while one was open for 29% of the time, Pallas kernels for 0%

profile of v1, /device:TPU:0, one launch (start us, length us, event | category | flops | bytes accessed | tf_op | source)
XLA Modules:
  0.0 249.2 jit_solution(5837964888765551572)
XLA Ops:
  6.5 0.7 all-gather.6.cloned.1.call-update
  7.3 0.0 all-gather.10.cloned.1.call-start
  7.3 59.4 %all-gather.6.cloned.1.call-done = bf16[1280,960]{1,0:T(8,128)(2,1)} async-done(((bf16[160,960]{1,0:T(8,128)(2,1)}), bf16[1280,960]{1,0:T(8,128)(2,1)}) %all-gather.6.cloned.1.call-update) | async-done | bytes 2457616 | tf_op jit(solution)/shard_map/all_gather | solution.py:38
  66.7 0.0 all-gather.8.cloned.1.call-start
  66.8 33.0 %all_gather.22 = bf16[1280,320]{1,0:T(8,128)(2,1)S(1)} all-gather(bf16[160,320]{1,0:T(8,128)(2,1)S(1)} %copy-done.3), channel_id=1, replica_groups=mesh['pipe'=4,'tensor'=8] {'tensor'}, dimensions={0}, use_global_device_ids=true | all-gather | bytes 921600 | tf_op jit(solution)/shard_map/all_gather | solution.py:68
  99.8 1.3 copy.58
  101.1 0.6 and_select_fusion.1
  101.7 0.2 select_reduce_fusion.3
  101.9 0.1 select_reduce_fusion.5
  102.0 0.2 reduce-window.8
  102.2 0.6 dynamic-slice
  103.4 0.2 dynamic-update-slice
  103.7 8.6 %all-reduce = s32[64]{0:T(128)S(1)} all-reduce(s32[64]{0:T(128)S(1)} %dynamic-update-slice), channel_id=2, replica_groups=mesh['pipe'=4,'tensor'=8] {'tensor'}, use_global_device_ids=true, to_apply=%add | all-reduce | flops 64 | bytes 512
  112.2 0.1 reshape.171
  112.3 0.1 select_reduce_fusion
  112.4 0.1 select_reduce_fusion.1
  112.5 0.2 select_reduce_fusion.4
  112.7 0.1 fusion.25
  112.8 0.1 select_reduce_fusion.2
  112.9 0.1 select_n.69
  113.0 0.7 copy.50
  113.7 4.5 %all-to-all-start = ((s32[16,8,1]{0,2,1:T(1,128)}), s32[16,8,1]{0,2,1:T(1,128)S(1)}, u32[]{:S(2)}, u32[]{:S(2)}) async-start(s32[16,8,1]{0,2,1:T(1,128)} %copy.50), calls=%async_computation | async-start | bytes 8192 | tf_op jit(solution)/shard_map/all_to_all | solution.py:100
  118.2 0.1 eq.67
  118.3 0.6 iota_compare_fusion.3
  118.9 0.7 add_compare_fusion
  119.6 0.3 fusion.3
  119.9 0.2 compare_and_fusion
  120.2 16.9 %all-gather.10.cloned.1.call-done = bf16[5120,960]{1,0:T(8,128)(2,1)} async-done(((bf16[1280,960]{1,0:T(8,128)(2,1)}), bf16[5120,960]{1,0:T(8,128)(2,1)}) %all-gather.10.cloned.1.call-update) | async-done | bytes 9830416 | tf_op jit(solution)/shard_map/all_gather | solution.py:41
  137.0 17.1 %copy.61 = bf16[4,1280,960]{1,0,2:T(4,128)(2,1)} copy(bf16[4,1280,960]{2,1,0:T(8,128)(2,1)} %bitcast.24) | data formatting | bytes 19660800 | tf_op jit(solution)/shard_map/all_gather | solution.py:41
  154.2 8.9 %copy.52 = bf16[1280,4,960]{0,2,1:T(8,128)(2,1)} copy(bf16[1280,4,960]{0,1,2:T(4,128)(2,1)} %bitcast.23) | data formatting | bytes 19660800 | tf_op jit(solution)/shard_map/reshape | solution.py:41
  163.0 9.5 %convolution_convert_fusion.1 = bf16[512,3840]{1,0:T(8,128)(2,1)S(1)} fusion(bf16[1280,3840]{0,1:T(8,128)(2,1)} %bitcast.25, bf16[512,1280]{1,0:T(8,128)(2,1)S(1)} %copy-done.1, f32[1280]{0:T(1024)S(1)} %copy-done.7, f32[512]{0:T(512)S(1)} %add_rsqrt_fusion.1), kind=kOutput, calls=%fused_computation.2 | convolution fusion | flops 5037752320 | bytes 15080448 | tf_op jit(solution)/shard_map/dot_general | solution.py:39
  172.6 1.3 fusion.26
  173.9 4.1 %reshape.165 = bf16[8,64,16,80]{3,2,1,0:T(8,128)(2,1)} reshape(bf16[512,1280]{1,0:T(8,128)(2,1)S(1)} %get-tuple-element.7) | data formatting | bytes 2621440 | tf_op jit(solution)/shard_map/reshape | solution.py:48
  178.0 4.1 %reshape.167 = bf16[8,64,16,80]{3,2,1,0:T(8,128)(2,1)S(1)} reshape(bf16[512,1280]{1,0:T(8,128)(2,1)} %get-tuple-element.8) | data formatting | bytes 2621440 | tf_op jit(solution)/shard_map/reshape | solution.py:48
  182.1 4.1 %reshape.166 = bf16[8,64,16,80]{3,2,1,0:T(8,128)(2,1)} reshape(bf16[512,1280]{1,0:T(8,128)(2,1)S(1)} %get-tuple-element.9) | data formatting | bytes 2621440 | tf_op jit(solution)/shard_map/reshape | solution.py:48
  186.2 2.8 %fusion.7 = f32[8,16,64,64]{2,3,1,0:T(8,128)S(1)} fusion(bf16[8,64,16,80]{3,2,1,0:T(8,128)(2,1)S(1)} %reshape.167, bf16[8,64,16,80]{3,2,1,0:T(8,128)(2,1)} %reshape.166), kind=kOutput, calls=%fused_computation.19 | convolution fusion | flops 83886080 | bytes 4718592 | tf_op jit(solution)/shard_map/tqhd,tkhd->thqk/dot_general | solution.py:53
  189.0 1.7 fusion.27
  190.7 1.2 convolution_bitcast_fusion
  191.9 1.4 copy.57
  193.3 3.3 %reshape.168 = bf16[512,1280]{1,0:T(8,128)(2,1)} reshape(bf16[8,64,16,80]{3,2,1,0:T(8,128)(2,1)S(1)} %copy.57) | data formatting | bytes 2621440 | tf_op jit(solution)/shard_map/reshape | solution.py:66
  196.6 4.4 %multiply_reduce_fusion = (f32[512]{0:T(512)S(1)}, f32[512,1280]{1,0:T(8,128)S(1)}) fusion(bf16[1280,1280]{0,1:T(8,128)(2,1)} %all-gather.8.cloned.1.call-done, bf16[512,1280]{1,0:T(8,128)(2,1)} %reshape.168, pred[512]{0:T(512)(128)(4,1)S(1)} %iota_compare_fusion.3, bf16[512,1280]{1,0:T(8,128)(2,1)S(1)} %copy-done.2), kind=kOutput, calls=%fused_computation.15 | convolution fusion | flops 1680997888 | bytes 8522240 | tf_op jit(solution)/shard_map/dot_general | solution.py:69
  201.0 0.3 multiply_convert_fusion
  201.3 0.8 reshape_reshape.3
  202.1 1.8 copy.59
  203.9 5.4 %all-to-all-start.1 = ((bf16[16,8,5120]{2,0,1:T(8,128)(2,1)}), bf16[16,8,5120]{2,0,1:T(8,128)(2,1)S(1)}, u32[]{:S(2)}, u32[]{:S(2)}) async-start(bf16[16,8,5120]{2,0,1:T(8,128)(2,1)} %copy.59), calls=%async_computation.1 | async-start | bytes 2621440 | tf_op jit(solution)/shard_map/all_to_all | solution.py:99
  209.3 0.1 reshape.162
  209.4 31.7 %all-to-all-done.1 = bf16[16,8,5120]{2,0,1:T(8,128)(2,1)S(1)} async-done(((bf16[16,8,5120]{2,0,1:T(8,128)(2,1)}), bf16[16,8,5120]{2,0,1:T(8,128)(2,1)S(1)}, u32[]{:S(2)}, u32[]{:S(2)}) %all-to-all-start.1) | async-done | bytes 1310752 | tf_op jit(solution)/shard_map/all_to_all | solution.py:99
  241.1 1.6 fusion.1
  (35 shorter events, 0.2 us)
Async XLA Ops:
  6.5 60.2 %copy-start.3 = (bf16[160,320]{1,0:T(8,128)(2,1)S(1)}, bf16[160,320]{1,0:T(8,128)(2,1)}, u32[]{:S(2)}) copy-start(bf16[160,320]{1,0:T(8,128)(2,1)} %param.11) | copy-start | bytes 307204
  6.5 60.1 %all-gather.6.cloned.1.call-start = ((), (), s32[]{:S(2)}) async-start(), calls=%async_computation.2 | async-start | bytes 2949120 | tf_op jit(solution)/shard_map/all_gather | solution.py:38
  7.3 129.8 %all-gather.10.cloned.1.call-start = ((), (), s32[]{:S(2)}) async-start(), calls=%async_computation.4 | async-start | bytes 13107200 | tf_op jit(solution)/shard_map/all_gather | solution.py:41
  66.7 34.4 %copy-start.8 = (s32[4]{0:T(128)S(1)}, s32[4]{0:T(128)}, u32[]{:S(2)}) copy-start(s32[4]{0:T(128)} %param.14) | copy-start | bytes 52
  66.7 35.0 %copy-start.6 = (s32[4]{0:T(128)S(1)}, s32[4]{0:T(128)}, u32[]{:S(2)}) copy-start(s32[4]{0:T(128)} %param.15) | copy-start | bytes 52
  66.7 35.5 %copy-start.9 = (u32[32]{0:T(128)S(1)}, u32[32]{0:T(128)}, u32[]{:S(2)}) copy-start(u32[32]{0:T(128)} %constant.61) | copy-start | bytes 388
  66.7 51.5 %copy-start.5 = (s32[512]{0:T(512)S(1)}, s32[512]{0:T(512)}, u32[]{:S(2)}) copy-start(s32[512]{0:T(512)} %param.13) | copy-start | bytes 6148
  66.7 52.9 %copy-start.1 = (bf16[512,1280]{1,0:T(8,128)(2,1)S(1)}, bf16[512,1280]{1,0:T(8,128)(2,1)}, u32[]{:S(2)}) copy-start(bf16[512,1280]{1,0:T(8,128)(2,1)} %param.8) | copy-start | bytes 3932164
  66.7 129.9 %all-gather.8.cloned.1.call-start = ((), (), s32[]{:S(2)}) async-start(), calls=%async_computation.3 | async-start | bytes 4096000 | tf_op jit(solution)/shard_map/all_gather | solution.py:71
  113.7 90.2 %all-to-all-start = ((s32[16,8,1]{0,2,1:T(1,128)}), s32[16,8,1]{0,2,1:T(1,128)S(1)}, u32[]{:S(2)}, u32[]{:S(2)}) async-start(s32[16,8,1]{0,2,1:T(1,128)} %copy.50), calls=%async_computation | async-start | bytes 8192 | tf_op jit(solution)/shard_map/all_to_all | solution.py:100
  154.1 8.9 %copy-start.7 = (f32[1280]{0:T(1024)S(1)}, f32[1280]{0:T(1024)}, u32[]{:S(2)}) copy-start(f32[1280]{0:T(1024)} %param.9) | copy-start | bytes 15364
  189.0 1.7 copy-start
  193.3 3.3 %copy-start.2 = (bf16[512,1280]{1,0:T(8,128)(2,1)S(1)}, bf16[512,1280]{1,0:T(8,128)(2,1)}, u32[]{:S(2)}) copy-start(bf16[512,1280]{1,0:T(8,128)(2,1)} %param.8) | copy-start | bytes 3932164
  196.6 4.4 %copy-start.4 = (f32[1280]{0:T(1024)S(1)}, f32[1280]{0:T(1024)}, u32[]{:S(2)}) copy-start(f32[1280]{0:T(1024)} %param.12) | copy-start | bytes 15364
  203.9 37.2 %all-to-all-start.1 = ((bf16[16,8,5120]{2,0,1:T(8,128)(2,1)}), bf16[16,8,5120]{2,0,1:T(8,128)(2,1)S(1)}, u32[]{:S(2)}, u32[]{:S(2)}) async-start(bf16[16,8,5120]{2,0,1:T(8,128)(2,1)} %copy.59), calls=%async_computation.1 | async-start | bytes 2621440 | tf_op jit(solution)/shard_map/all_to_all | solution.py:99
Sparse Core Ops, SparseCore 0:
  9.5 57.1 all-gather.5
  68.2 68.7 all-gather.9
  138.6 29.2 all-gather.7
